TPU v7x, 32 devices: a whole 2x2x4 slice. The times are simulated.
32 devices in a mesh: grp: 2 (over x), scen: 16 (over z, y, core).
Axes of the slice: x: 2, y: 2, z: 4, core: 2. Of those that a mesh axis runs over, the one named last changes fastest.
Arguments:
- shocks: bfloat16 [32768, 2048], P(('grp', 'scen')), parts along dimension 0, may hold values from -8 to 8
- factor_sens: bfloat16 [2048, 1024], replicated, may hold values from -0.13258252 to 0.13258252
- notional: float32 [1024], replicated, may hold values from -0.25 to 0.25
- moneyness: float32 [1024], replicated, may hold values from -2 to 2
- desk_entity: int32 [64], replicated, may hold values from 0 to 7
- scenario_counts: int32 [32], P(('grp', 'scen')), parts along dimension 0, may hold values from 256 to 1024, as said below
- candidate_ids: int32 [2048], P('grp'), parts along dimension 0, may hold values from 0 to 16383, as said below
Outputs:
- tail_losses: float32 [512], P('grp'), parts along dimension 0
- cand_entity: float32 [2048, 8], P(('grp', 'scen')), parts along dimension 0
There are 2 independent parts, one for each index of `grp`. A program takes and returns all parts, laid end to end along the dimension named above; an argument that names none is the same for every part. Nothing has to cross between parts.
Inputs may be any that keep to these rules, and one draw needn't show every extreme that they name: `scenario_counts`: every block has at least 256 valid scenarios; some block in every draw is full. `candidate_ids`: each id b * 1024 + j names a valid scenario: j is below scenario_counts[b].
All inputs are finite; a program needn't handle non-finite values.
Results may differ from a plain program's by a relative error of at most 0.0003.
Values sent between devices are 32-bit elements; how exact they have to be, the bound alone decides.
A program may use at most 128 MiB of HBM per device.

v0:
```python
import jax
import jax.numpy as jnp
from jax import lax
from jax.sharding import PartitionSpec as P

K = 64
INSTR = 16
ENT = 8
TOPK = 256


def price(rows, factor_sens, notional, moneyness):
    value = jnp.dot(rows, factor_sens, preferred_element_type=jnp.float32)
    inst = notional * (jax.nn.softplus(value + moneyness) - jax.nn.softplus(moneyness))
    return jnp.sum(inst.reshape(rows.shape[0], K, INSTR), axis=2)


def body(shocks, factor_sens, notional, moneyness, desk_entity, scenario_counts, candidate_ids):
    slots = shocks.shape[0]
    count = scenario_counts[0]
    block_rows = min(256, slots)
    turns = slots // block_rows

    def one_block(step, desk_all):
        start = step * block_rows

        def active(unused):
            rows = lax.dynamic_slice_in_dim(shocks, start, block_rows, 0)
            return price(rows, factor_sens, notional, moneyness)

        def skipped(unused):
            return jnp.zeros((block_rows, K), jnp.float32)

        piece = lax.cond(start < count, active, skipped, 0)
        return lax.dynamic_update_slice_in_dim(desk_all, piece, start, 0)

    desk_pnl = lax.fori_loop(0, turns, one_block, jnp.zeros((slots, K), jnp.float32))
    loss = -jnp.sum(desk_pnl, axis=1)
    valid = jnp.arange(slots, dtype=jnp.int32) < count
    local_top = lax.top_k(jnp.where(valid, loss, jnp.float32(-1e30)), TOPK)[0]
    every_list = lax.all_gather(local_top, "scen", axis=0, tiled=True)
    tail_losses = lax.top_k(every_list, TOPK)[0]
    local_ids = candidate_ids - lax.axis_index("scen") * slots
    owned = (local_ids >= 0) & (local_ids < slots)
    clipped = jnp.clip(local_ids, 0, slots - 1)
    onehot = (desk_entity[:, None] == jnp.arange(ENT, dtype=jnp.int32)[None, :]).astype(jnp.float32)
    cand_pnl = lax.psum_scatter(
        jnp.where(owned[:, None], jnp.take(desk_pnl, clipped, axis=0), jnp.float32(0.0)),
        "scen",
        scatter_dimension=0,
        tiled=True,
    )
    cand_entity = -jnp.dot(cand_pnl, onehot, precision=lax.Precision.HIGHEST)
    return (tail_losses, cand_entity)


def solution(mesh):
    return jax.shard_map(
        body,
        mesh=mesh,
        in_specs=(P(("grp", "scen"), None), P(), P(), P(), P(), P(("grp", "scen")), P("grp")),
        out_specs=(P("grp"), P(("grp", "scen"), None)),
        check_vma=False,
    )
```

profile of v0, /device:TPU:0, one launch (start us, length us, event | category | flops | bytes accessed | tf_op | source)
XLA Modules:
  0.0 104.4 jit_solution(15786896003439924886)
XLA Ops:
  7.2 0.7 fusion.5
  7.9 0.7 compare_and_fusion.1
  8.6 25.0 %while.13 = (s32[]{:T(128)}, f32[1024,64]{0,1:T(8,128)S(1)}, s32[]{:T(128)}, f32[1024]{0:T(1024)}, bf16[1024,2048]{1,0:T(8,128)(2,1)}, /*index=5*/bf16[2048,1024...) while((s32[]{:T(128)}, f32[1024,64]{0,1:T(8,128)S(1)}, ...), condition=%wide.region_4.5_spmd, body=%wide.region_0.4_spmd.sunk | while | flops 1076353024 | bytes 9654531 | solution.py:37
  9.3 5.6 %conditional.2 = (f32[256,64]{0,1:T(8,128)S(1)}) conditional(s32[]{:T(128)} %convert_element_type.9, () %tuple.42, (f32[1024]{0:T(1024)}, s32[]{:T(128)}, bf16[1024,2048]{1,0:T(8,128)(2,1)}, bf16[2048,1024]{1,0:T(8,128)(2,1)}, f32[1024]{0:T(1024)}) %tuple.43), branch_computations={%region_1.0_spmd, %region_2.3_spmd} | conditional | flops 1076353024 | bytes 9523246 | solution.py:34
  9.3 0.7 compare_select_fusion.1
  10.0 4.3 %fusion.1 = f32[256,1024]{1,0:T(8,128)S(1)} fusion(bf16[2048,1024]{1,0:T(8,128)(2,1)} %get-tuple-element.137, bf16[1024,2048]{1,0:T(8,128)(2,1)} %get-tuple-element.135, s32[]{:T(128)S(6)} %select_n.27, f32[1024]{0:T(1024)S(1)} %compare_select_fusion.1, f32[1024]{0:T(1024)} %get-tuple-element.138, f32[1024]{0:T(1024)} %get-tuple-element.134), kind=kOutput, calls=%fused_computation.4 | convolution fusion | flops 1076101120 | bytes 6303748 | tf_op jit(solution)/shard_map/while/body/eval_jaxpr/cond/branch_1_fun/dot_general | solution.py:13
  14.3 0.3 copy.10
  14.7 0.2 bitcast_reduce_fusion
  15.5 5.6 %conditional.2 = (f32[256,64]{0,1:T(8,128)S(1)}) conditional(s32[]{:T(128)} %convert_element_type.9, () %tuple.42, (f32[1024]{0:T(1024)}, s32[]{:T(128)}, bf16[1024,2048]{1,0:T(8,128)(2,1)}, bf16[2048,1024]{1,0:T(8,128)(2,1)}, f32[1024]{0:T(1024)}) %tuple.43), branch_computations={%region_1.0_spmd, %region_2.3_spmd} | conditional | flops 1076353024 | bytes 9523246 | solution.py:34
  15.6 0.7 compare_select_fusion.1
  16.3 4.3 %fusion.1 = f32[256,1024]{1,0:T(8,128)S(1)} fusion(bf16[2048,1024]{1,0:T(8,128)(2,1)} %get-tuple-element.137, bf16[1024,2048]{1,0:T(8,128)(2,1)} %get-tuple-element.135, s32[]{:T(128)S(6)} %select_n.27, f32[1024]{0:T(1024)S(1)} %compare_select_fusion.1, f32[1024]{0:T(1024)} %get-tuple-element.138, f32[1024]{0:T(1024)} %get-tuple-element.134), kind=kOutput, calls=%fused_computation.4 | convolution fusion | flops 1076101120 | bytes 6303748 | tf_op jit(solution)/shard_map/while/body/eval_jaxpr/cond/branch_1_fun/dot_general | solution.py:13
  20.6 0.3 copy.10
  20.9 0.2 bitcast_reduce_fusion
  21.8 5.6 %conditional.2 = (f32[256,64]{0,1:T(8,128)S(1)}) conditional(s32[]{:T(128)} %convert_element_type.9, () %tuple.42, (f32[1024]{0:T(1024)}, s32[]{:T(128)}, bf16[1024,2048]{1,0:T(8,128)(2,1)}, bf16[2048,1024]{1,0:T(8,128)(2,1)}, f32[1024]{0:T(1024)}) %tuple.43), branch_computations={%region_1.0_spmd, %region_2.3_spmd} | conditional | flops 1076353024 | bytes 9523246 | solution.py:34
  21.8 0.7 compare_select_fusion.1
  22.5 4.3 %fusion.1 = f32[256,1024]{1,0:T(8,128)S(1)} fusion(bf16[2048,1024]{1,0:T(8,128)(2,1)} %get-tuple-element.137, bf16[1024,2048]{1,0:T(8,128)(2,1)} %get-tuple-element.135, s32[]{:T(128)S(6)} %select_n.27, f32[1024]{0:T(1024)S(1)} %compare_select_fusion.1, f32[1024]{0:T(1024)} %get-tuple-element.138, f32[1024]{0:T(1024)} %get-tuple-element.134), kind=kOutput, calls=%fused_computation.4 | convolution fusion | flops 1076101120 | bytes 6303748 | tf_op jit(solution)/shard_map/while/body/eval_jaxpr/cond/branch_1_fun/dot_general | solution.py:13
  26.8 0.3 copy.10
  27.2 0.2 bitcast_reduce_fusion
  28.1 5.6 %conditional.2 = (f32[256,64]{0,1:T(8,128)S(1)}) conditional(s32[]{:T(128)} %convert_element_type.9, () %tuple.42, (f32[1024]{0:T(1024)}, s32[]{:T(128)}, bf16[1024,2048]{1,0:T(8,128)(2,1)}, bf16[2048,1024]{1,0:T(8,128)(2,1)}, f32[1024]{0:T(1024)}) %tuple.43), branch_computations={%region_1.0_spmd, %region_2.3_spmd} | conditional | flops 1076353024 | bytes 9523246 | solution.py:34
  28.1 0.7 compare_select_fusion.1
  28.8 4.3 %fusion.1 = f32[256,1024]{1,0:T(8,128)S(1)} fusion(bf16[2048,1024]{1,0:T(8,128)(2,1)} %get-tuple-element.137, bf16[1024,2048]{1,0:T(8,128)(2,1)} %get-tuple-element.135, s32[]{:T(128)S(6)} %select_n.27, f32[1024]{0:T(1024)S(1)} %compare_select_fusion.1, f32[1024]{0:T(1024)} %get-tuple-element.138, f32[1024]{0:T(1024)} %get-tuple-element.134), kind=kOutput, calls=%fused_computation.4 | convolution fusion | flops 1076101120 | bytes 6303748 | tf_op jit(solution)/shard_map/while/body/eval_jaxpr/cond/branch_1_fun/dot_general | solution.py:13
  33.1 0.3 copy.10
  33.4 0.2 bitcast_reduce_fusion
  33.7 0.2 copy.12
  33.9 2.8 %gather_fusion = f32[1024,64]{1,0:T(8,128)S(1)} fusion(f32[1024,64]{1,0:T(8,128)S(1)} %copy.12, s32[1024]{0:T(1024)S(1)} %fusion.5), kind=kCustom, calls=%fused_computation | custom fusion | bytes 528384 | tf_op jit(solution)/shard_map/jit(_take)/gather | solution.py:48
  36.7 1.1 %select_select_fusion = f32[1024,64]{1,0:T(8,128)} fusion(f32[1024,64]{1,0:T(8,128)S(1)} %gather_fusion, pred[1024]{0:T(1024)(128)(4,1)S(1)} %get-tuple-element.177, pred[1024]{0:T(1024)(128)(4,1)S(1)} %get-tuple-element.176), kind=kLoop, calls=%fused_computation.11 | loop fusion | flops 131072 | bytes 526336 | tf_op jit(solution)/shard_map/jit(_where)/select_n | solution.py:48
  38.5 4.4 %top_k.14 = (f32[1024]{0:T(1024)S(1)}, s32[1024]{0:T(1024)}) sort(f32[1024]{0:T(1024)S(1)} %negate_select_fusion, s32[1024]{0:T(1024)S(1)} %iota.14), dimensions={0}, to_apply=%region_6.7 | sort | flops 10240 | bytes 16384 | tf_op jit(solution)/shard_map/top_k | solution.py:40
  43.0 20.1 %all-gather = f32[16,1,256]{2,1,0:T(1,128)S(1)} all-gather(f32[1,1,256]{2,1,0:T(1,128)S(1)} %bitcast.9), channel_id=1, replica_groups=mesh['grp'=2,'scen'=16] {'scen'}, dimensions={0}, use_global_device_ids=true | all-gather | bytes 17408 | tf_op jit(solution)/shard_map/all_gather | solution.py:41
  63.1 5.9 %top_k.20 = (f32[4096]{0:T(1024)S(1)}, s32[4096]{0:T(1024)}) sort(f32[4096]{0:T(1024)S(1)} %bitcast.8, s32[4096]{0:T(1024)S(1)} %iota.15), dimensions={0}, to_apply=%region_7.8 | sort | flops 49152 | bytes 65536 | tf_op jit(solution)/shard_map/top_k | solution.py:42
  69.0 0.6 top_k.21
  69.5 26.5 %reduce-scatter.2.cloned.1.call-done = f32[64,64]{1,0:T(8,128)} async-done(((f32[1024,64]{1,0:T(8,128)}), f32[64,64]{1,0:T(8,128)}) %reduce-scatter.2.cloned.1.call-update) | async-done | bytes 16400 | tf_op jit(solution)/shard_map/reduce_scatter | solution.py:47
  96.0 1.6 %convolution_negate_fusion = f32[64,8]{0,1:T(8,128)} fusion(f32[64,64]{1,0:T(8,128)} %reduce-scatter.2.cloned.1.call-done, s32[64]{0:T(128)S(1)} %copy-done), kind=kOutput, calls=%fused_computation.10 | convolution fusion | flops 394240 | bytes 18688 | tf_op jit(solution)/shard_map/dot_general | solution.py:53
  (14 shorter events, 0.2 us)
Async XLA Ops:
  7.2 88.8 %reduce-scatter.2.cloned.1.call-start = ((), (), s32[]{:S(2)}) async-start(), calls=%async_computation.1 | async-start | bytes 557056 | tf_op jit(solution)/shard_map/reduce_scatter | solution.py:47
  33.7 62.3 %copy-start = (s32[64]{0:T(128)S(1)}, s32[64]{0:T(128)}, u32[]{:S(2)}) copy-start(s32[64]{0:T(128)} %param.15) | copy-start | bytes 772
Sparse Core Ops, SparseCore 0:
  38.0 57.9 reduce-scatter.1
where the time goes:
time: 105 us; the launch traced here: 104 us
  waiting for transfers between devices  26.5 us (25%)
  blocking collectives  20.1 us (19%)
  matrix products  18.8 us (18%)
  other arithmetic  16.4 us (16%)
  between operations  14.7 us (14%)
  local copies, waits for them, and re-layouts  4.97 us (5%)
  loops' own time  2.9 us (3%)
    reduce_scatter x1, waiting for transfers between devices, body(): lax.psum_scatter(jnp.where(owned[:, None], jnp.take(desk_pnl, clipped, ax...  26.5 us
    all_gather x1, blocking collectives, body(): every_list = lax.all_gather(local_top, 'scen', axis=0, tiled=True)  20.1 us
    dot_general x4, matrix products, price(): value = jnp.dot(rows, factor_sens, preferred_element_type=jnp.float32)  17.2 us
    top_k x1, other arithmetic, body(): tail_losses = lax.top_k(every_list, TOPK)[0]  5.87 us
    top_k x1, other arithmetic, body(): local_top = lax.top_k(jnp.where(valid, loss, jnp.float32(-1e+30)), TOPK)[0]  4.43 us
    gather x1, local copies, waits for them, and re-layouts, body(): jnp.take(desk_pnl, clipped, axis=0)  2.8 us
    select_n x4, other arithmetic, price(): jax.nn.softplus(moneyness)  2.8 us
    another operation x1, loops' own time, body(): lax.fori_loop(0, turns, one_block, jnp.zeros((slots, K), jnp.float32))  2.73 us
  transfers between devices with their start and end apart: 1, of which 1 were waited for; matrix products, arithmetic and copies ran while one was open for 10% of the time, Pallas kernels for 0%

commit v1 on v0

--- a/solution.py
+++ b/solution.py
@@ -1,12 +1,40 @@
+import functools
 import jax
 import jax.numpy as jnp
 from jax import lax
 from jax.sharding import PartitionSpec as P
+from jax.lax import axis_index, ppermute, psum
 
 K = 64
 INSTR = 16
 ENT = 8
 TOPK = 256
+
+
+def keys_switch(array_in, array_axis):
+    piece_out = list(array_in.shape[1:])
+    piece_out[array_axis] *= array_in.shape[0]
+    return jnp.moveaxis(array_in, 0, array_axis).reshape(piece_out)
+
+
+def trace_the_case(sheet, dev_axis):
+    carry = sheet[None]
+    width = psum(1, dev_axis)
+    for tick in range(width.bit_length() - 1):
+        ready = 1 << tick
+        spare = ppermute(carry, dev_axis, [(h, h ^ ready) for h in range(width)])
+        inter = jnp.stack([carry, spare])
+        current_block = axis_index(dev_axis) >> tick & 1
+        carry = jnp.where(current_block == 0, inter, inter[::-1]).reshape(-1, *sheet.shape)
+    return carry
+
+
+def remake_squares(point, sample, dim_no):
+    b_next = trace_the_case(point, sample)
+    return keys_switch(b_next, dim_no)
+
+
+cube_balance = functools.partial(remake_squares, sample="scen", dim_no=0)
 
 
 def price(rows, factor_sens, notional, moneyness):
@@ -38,7 +66,7 @@
     loss = -jnp.sum(desk_pnl, axis=1)
     valid = jnp.arange(slots, dtype=jnp.int32) < count
     local_top = lax.top_k(jnp.where(valid, loss, jnp.float32(-1e30)), TOPK)[0]
-    every_list = lax.all_gather(local_top, "scen", axis=0, tiled=True)
+    every_list = cube_balance(local_top)
     tail_losses = lax.top_k(every_list, TOPK)[0]
     local_ids = candidate_ids - lax.axis_index("scen") * slots
     owned = (local_ids >= 0) & (local_ids < slots)

time: 105 us -> 112 us (1.067)
  waiting for transfers between devices: 26.5 us -> 48.6 us
  blocking collectives: 20.1 us -> 0 us
  starting transfers between devices: 0.04 us -> 6.3 us
  other arithmetic: 16.4 us -> 15.1 us
    all_gather x1 -> x0, blocking collectives: 20.1 us -> none  [body(): every_list = lax.all_gather(local_top, 'scen', axis=0, tiled=True)]
    reduce_scatter x1, waiting for transfers between devices: 26.5 us -> 43.6 us  [body(): lax.psum_scatter(jnp.where(owned[:, None], jnp.take(desk_pnl, clipped, ax...]
    ppermute x0 -> x4, starting transfers between devices: none -> 6.26 us  [trace_the_case(): spare = ppermute(carry, dev_axis, [(h, h ^ ready) for h in range(width)])]
    ppermute x0 -> x4, waiting for transfers between devices: none -> 5.06 us  [trace_the_case(): spare = ppermute(carry, dev_axis, [(h, h ^ ready) for h in range(width)])]
  transfers between devices with their start and end apart: 1 -> 5, of which waited for: 1 -> 4; matrix products, arithmetic and copies ran while one was open for 10% -> 10% of each run, Pallas kernels for 0% -> 0%
where the time goes in v1:
time: 112 us
  waiting for transfers between devices  48.6 us (43%)
  matrix products  18.8 us (17%)
  other arithmetic  15.1 us (13%)
  between operations  14.8 us (13%)
  starting transfers between devices  6.3 us (6%)
  local copies, waits for them, and re-layouts  5.09 us (5%)
  loops' own time  2.9 us (3%)
    reduce_scatter x1, waiting for transfers between devices, body(): lax.psum_scatter(jnp.where(owned[:, None], jnp.take(desk_pnl, clipped, ax...  43.6 us
    dot_general x4, matrix products, price(): value = jnp.dot(rows, factor_sens, preferred_element_type=jnp.float32)  17.2 us
    ppermute x4, starting transfers between devices, trace_the_case(): spare = ppermute(carry, dev_axis, [(h, h ^ ready) for h in range(width)])  6.26 us
    top_k x1, other arithmetic, body(): tail_losses = lax.top_k(every_list, TOPK)[0]  5.87 us
    ppermute x4, waiting for transfers between devices, trace_the_case(): spare = ppermute(carry, dev_axis, [(h, h ^ ready) for h in range(width)])  5.06 us
    top_k x1, other arithmetic, body(): local_top = lax.top_k(jnp.where(valid, loss, jnp.float32(-1e+30)), TOPK)[0]  4.43 us
    gather x1, local copies, waits for them, and re-layouts, body(): jnp.take(desk_pnl, clipped, axis=0)  2.81 us
    select_n x4, other arithmetic, price(): jax.nn.softplus(moneyness)  2.8 us
  transfers between devices with their start and end apart: 5, of which 4 were waited for; matrix products, arithmetic and copies ran while one was open for 10% of the time, Pallas kernels for 0%

profile of v1, /device:TPU:0, one launch (start us, length us, event | category | flops | bytes accessed | tf_op | source)
XLA Modules:
  0.0 111.7 jit_solution(10839767022200876874)
XLA Ops:
  7.9 25.0 %while.13 = (s32[]{:T(128)}, f32[1024,64]{0,1:T(8,128)S(1)}, s32[]{:T(128)}, f32[1024]{0:T(1024)}, bf16[1024,2048]{1,0:T(8,128)(2,1)}, /*index=5*/bf16[2048,1024...) while((s32[]{:T(128)}, f32[1024,64]{0,1:T(8,128)S(1)}, ...), condition=%wide.region_4.5_spmd, body=%wide.region_0.4_spmd.sunk | while | flops 1076353024 | bytes 9654531 | solution.py:65
  8.6 5.6 %conditional.2 = (f32[256,64]{0,1:T(8,128)S(1)}) conditional(s32[]{:T(128)} %convert_element_type.9, () %tuple.43, (f32[1024]{0:T(1024)}, s32[]{:T(128)}, bf16[1024,2048]{1,0:T(8,128)(2,1)}, bf16[2048,1024]{1,0:T(8,128)(2,1)}, f32[1024]{0:T(1024)}) %tuple.44), branch_computations={%region_1.0_spmd, %region_2.3_spmd} | conditional | flops 1076353024 | bytes 9523246 | solution.py:62
  8.6 0.7 compare_select_fusion.1
  9.3 4.3 %fusion.1 = f32[256,1024]{1,0:T(8,128)S(1)} fusion(bf16[2048,1024]{1,0:T(8,128)(2,1)} %get-tuple-element.137, bf16[1024,2048]{1,0:T(8,128)(2,1)} %get-tuple-element.135, s32[]{:T(128)S(6)} %select_n.51, f32[1024]{0:T(1024)S(1)} %compare_select_fusion.1, f32[1024]{0:T(1024)} %get-tuple-element.138, f32[1024]{0:T(1024)} %get-tuple-element.134), kind=kOutput, calls=%fused_computation.4 | convolution fusion | flops 1076101120 | bytes 6303748 | tf_op jit(solution)/shard_map/while/body/eval_jaxpr/cond/branch_1_fun/dot_general | solution.py:41
  13.6 0.3 copy.10
  14.8 5.6 %conditional.2 = (f32[256,64]{0,1:T(8,128)S(1)}) conditional(s32[]{:T(128)} %convert_element_type.9, () %tuple.43, (f32[1024]{0:T(1024)}, s32[]{:T(128)}, bf16[1024,2048]{1,0:T(8,128)(2,1)}, bf16[2048,1024]{1,0:T(8,128)(2,1)}, f32[1024]{0:T(1024)}) %tuple.44), branch_computations={%region_1.0_spmd, %region_2.3_spmd} | conditional | flops 1076353024 | bytes 9523246 | solution.py:62
  14.9 0.7 compare_select_fusion.1
  15.6 4.3 %fusion.1 = f32[256,1024]{1,0:T(8,128)S(1)} fusion(bf16[2048,1024]{1,0:T(8,128)(2,1)} %get-tuple-element.137, bf16[1024,2048]{1,0:T(8,128)(2,1)} %get-tuple-element.135, s32[]{:T(128)S(6)} %select_n.51, f32[1024]{0:T(1024)S(1)} %compare_select_fusion.1, f32[1024]{0:T(1024)} %get-tuple-element.138, f32[1024]{0:T(1024)} %get-tuple-element.134), kind=kOutput, calls=%fused_computation.4 | convolution fusion | flops 1076101120 | bytes 6303748 | tf_op jit(solution)/shard_map/while/body/eval_jaxpr/cond/branch_1_fun/dot_general | solution.py:41
  19.9 0.3 copy.10
  21.1 5.6 %conditional.2 = (f32[256,64]{0,1:T(8,128)S(1)}) conditional(s32[]{:T(128)} %convert_element_type.9, () %tuple.43, (f32[1024]{0:T(1024)}, s32[]{:T(128)}, bf16[1024,2048]{1,0:T(8,128)(2,1)}, bf16[2048,1024]{1,0:T(8,128)(2,1)}, f32[1024]{0:T(1024)}) %tuple.44), branch_computations={%region_1.0_spmd, %region_2.3_spmd} | conditional | flops 1076353024 | bytes 9523246 | solution.py:62
  21.1 0.7 compare_select_fusion.1
  21.8 4.3 %fusion.1 = f32[256,1024]{1,0:T(8,128)S(1)} fusion(bf16[2048,1024]{1,0:T(8,128)(2,1)} %get-tuple-element.137, bf16[1024,2048]{1,0:T(8,128)(2,1)} %get-tuple-element.135, s32[]{:T(128)S(6)} %select_n.51, f32[1024]{0:T(1024)S(1)} %compare_select_fusion.1, f32[1024]{0:T(1024)} %get-tuple-element.138, f32[1024]{0:T(1024)} %get-tuple-element.134), kind=kOutput, calls=%fused_computation.4 | convolution fusion | flops 1076101120 | bytes 6303748 | tf_op jit(solution)/shard_map/while/body/eval_jaxpr/cond/branch_1_fun/dot_general | solution.py:41
  26.1 0.3 copy.10
  27.3 5.6 %conditional.2 = (f32[256,64]{0,1:T(8,128)S(1)}) conditional(s32[]{:T(128)} %convert_element_type.9, () %tuple.43, (f32[1024]{0:T(1024)}, s32[]{:T(128)}, bf16[1024,2048]{1,0:T(8,128)(2,1)}, bf16[2048,1024]{1,0:T(8,128)(2,1)}, f32[1024]{0:T(1024)}) %tuple.44), branch_computations={%region_1.0_spmd, %region_2.3_spmd} | conditional | flops 1076353024 | bytes 9523246 | solution.py:62
  27.4 0.7 compare_select_fusion.1
  28.1 4.3 %fusion.1 = f32[256,1024]{1,0:T(8,128)S(1)} fusion(bf16[2048,1024]{1,0:T(8,128)(2,1)} %get-tuple-element.137, bf16[1024,2048]{1,0:T(8,128)(2,1)} %get-tuple-element.135, s32[]{:T(128)S(6)} %select_n.51, f32[1024]{0:T(1024)S(1)} %compare_select_fusion.1, f32[1024]{0:T(1024)} %get-tuple-element.138, f32[1024]{0:T(1024)} %get-tuple-element.134), kind=kOutput, calls=%fused_computation.4 | convolution fusion | flops 1076101120 | bytes 6303748 | tf_op jit(solution)/shard_map/while/body/eval_jaxpr/cond/branch_1_fun/dot_general | solution.py:41
  32.4 0.3 copy.10
  33.0 4.4 %top_k.14 = (f32[1024]{0:T(1024)S(1)}, s32[1024]{0:T(1024)}) sort(f32[1024]{0:T(1024)S(1)} %negate_select_fusion, s32[1024]{0:T(1024)S(1)} %iota.14), dimensions={0}, to_apply=%region_6.7 | sort | flops 10240 | bytes 16384 | tf_op jit(solution)/shard_map/top_k | solution.py:68
  37.4 0.5 collective-permute-start
  38.0 0.8 collective-permute-done
  38.9 2.9 %collective-permute-start.1 = (f32[2,256]{1,0:T(2,128)S(1)}, f32[2,256]{1,0:T(2,128)S(1)}, u32[]{:S(2)}, u32[]{:S(2)}) collective-permute-start(f32[2,256]{1,0:T(2,128)S(1)} %get-tuple-element.179), channel_id=1, source_target_pairs={{0,2},{1,3},{2,0},{3,1},{4,6},{5,7},{6,4},{7,5},{8,10},{9,11},{10,... | collective-permute-start | bytes 6152 | tf_op jit(solution)/shard_map/ppermute | solution.py:25
  41.8 0.2 copy.12
  42.0 2.8 %gather_fusion = f32[1024,64]{1,0:T(8,128)S(1)} fusion(f32[1024,64]{1,0:T(8,128)S(1)} %copy.12, s32[1024]{0:T(1024)S(1)} %fusion.6), kind=kCustom, calls=%fused_computation | custom fusion | bytes 528384 | tf_op jit(solution)/shard_map/jit(_take)/gather | solution.py:76
  44.8 1.6 %collective-permute-start.2 = (f32[4,256]{1,0:T(4,128)S(1)}, f32[4,256]{1,0:T(4,128)S(1)}, u32[]{:S(2)}, u32[]{:S(2)}) collective-permute-start(f32[4,256]{1,0:T(4,128)S(1)} %reshape.27), channel_id=1, source_target_pairs={{0,4},{1,5},{2,6},{3,7},{4,0},{5,1},{6,2},{7,3},{8,12},{9,13},{10,... | collective-permute-start | bytes 12296 | tf_op jit(solution)/shard_map/ppermute | solution.py:25
  46.5 1.1 %select_select_fusion = f32[1024,64]{1,0:T(8,128)} fusion(f32[1024,64]{1,0:T(8,128)S(1)} %gather_fusion, pred[1024]{0:T(1024)(128)(4,1)S(1)} %get-tuple-element.177, pred[1024]{0:T(1024)(128)(4,1)S(1)} %get-tuple-element.176), kind=kLoop, calls=%fused_computation.11 | loop fusion | flops 131072 | bytes 526336 | tf_op jit(solution)/shard_map/jit(_where)/select_n | solution.py:76
  47.7 0.9 collective-permute-done.2
  48.5 1.2 %collective-permute-start.3 = (f32[8,256]{1,0:T(8,128)S(1)}, f32[8,256]{1,0:T(8,128)S(1)}, u32[]{:S(2)}, u32[]{:S(2)}) collective-permute-start(f32[8,256]{1,0:T(8,128)S(1)} %reshape.28), channel_id=1, source_target_pairs={{0,8},{1,9},{2,10},{3,11},{4,12},{5,13},{6,14},{7,15},{8,0},{9,1},... | collective-permute-start | bytes 24584 | tf_op jit(solution)/shard_map/ppermute | solution.py:25
  49.8 3.4 %collective-permute-done.3 = f32[8,256]{1,0:T(8,128)S(1)} collective-permute-done((f32[8,256]{1,0:T(8,128)S(1)}, f32[8,256]{1,0:T(8,128)S(1)}, u32[]{:S(2)}, u32[]{:S(2)}) %collective-permute-start.3) | collective-permute-done | bytes 8224 | tf_op jit(solution)/shard_map/ppermute | solution.py:25
  53.2 5.9 %top_k.20 = (f32[4096]{0:T(1024)S(1)}, s32[4096]{0:T(1024)}) sort(f32[4096]{0:T(1024)S(1)} %bitcast.19, s32[4096]{0:T(1024)S(1)} %iota.15), dimensions={0}, to_apply=%region_7.8 | sort | flops 49152 | bytes 65536 | tf_op jit(solution)/shard_map/top_k | solution.py:70
  59.1 0.6 top_k.21
  59.6 43.6 %reduce-scatter.2.cloned.1.call-done = f32[64,64]{1,0:T(8,128)} async-done(((f32[1024,64]{1,0:T(8,128)}), f32[64,64]{1,0:T(8,128)}) %reduce-scatter.2.cloned.1.call-update) | async-done | bytes 16400 | tf_op jit(solution)/shard_map/reduce_scatter | solution.py:75
  103.2 1.6 %convolution_negate_fusion = f32[64,8]{0,1:T(8,128)} fusion(f32[64,64]{1,0:T(8,128)} %reduce-scatter.2.cloned.1.call-done, s32[64]{0:T(128)S(1)} %copy-done.1), kind=kOutput, calls=%fused_computation.10 | convolution fusion | flops 394240 | bytes 18688 | tf_op jit(solution)/shard_map/dot_general | solution.py:81
  (37 shorter events, 1.1 us)
Async XLA Ops:
  7.2 96.0 %reduce-scatter.2.cloned.1.call-start = ((), (), s32[]{:S(2)}) async-start(), calls=%async_computation.1 | async-start | bytes 557056 | tf_op jit(solution)/shard_map/reduce_scatter | solution.py:75
  7.9 30.1 %copy-start = (s32[1024]{0:T(1024)S(1)}, s32[1024]{0:T(1024)}, u32[]{:S(2)}) copy-start(s32[1024]{0:T(1024)} %param.17) | copy-start | bytes 12292
  32.9 70.3 %copy-start.1 = (s32[64]{0:T(128)S(1)}, s32[64]{0:T(128)}, u32[]{:S(2)}) copy-start(s32[64]{0:T(128)} %param.15) | copy-start | bytes 772
  37.4 1.3 %collective-permute-start = (f32[1,256]{1,0:T(1,128)S(1)}, f32[1,256]{1,0:T(1,128)S(1)}, u32[]{:S(2)}, u32[]{:S(2)}) collective-permute-start(f32[1,256]{1,0:T(1,128)S(1)} %bitcast.20), channel_id=1, source_target_pairs={{0,1},{1,0},{2,3},{3,2},{4,5},{5,4},{6,7},{7,6},{8,9},{9,8},{10,11... | collective-permute-start | bytes 3080 | tf_op jit(solution)/shard_map/ppermute | solution.py:25
  38.9 5.9 %collective-permute-start.1 = (f32[2,256]{1,0:T(2,128)S(1)}, f32[2,256]{1,0:T(2,128)S(1)}, u32[]{:S(2)}, u32[]{:S(2)}) collective-permute-start(f32[2,256]{1,0:T(2,128)S(1)} %get-tuple-element.179), channel_id=1, source_target_pairs={{0,2},{1,3},{2,0},{3,1},{4,6},{5,7},{6,4},{7,5},{8,10},{9,11},{10,... | collective-permute-start | bytes 6152 | tf_op jit(solution)/shard_map/ppermute | solution.py:25
  44.8 3.7 %collective-permute-start.2 = (f32[4,256]{1,0:T(4,128)S(1)}, f32[4,256]{1,0:T(4,128)S(1)}, u32[]{:S(2)}, u32[]{:S(2)}) collective-permute-start(f32[4,256]{1,0:T(4,128)S(1)} %reshape.27), channel_id=1, source_target_pairs={{0,4},{1,5},{2,6},{3,7},{4,0},{5,1},{6,2},{7,3},{8,12},{9,13},{10,... | collective-permute-start | bytes 12296 | tf_op jit(solution)/shard_map/ppermute | solution.py:25
  48.5 4.6 %collective-permute-start.3 = (f32[8,256]{1,0:T(8,128)S(1)}, f32[8,256]{1,0:T(8,128)S(1)}, u32[]{:S(2)}, u32[]{:S(2)}) collective-permute-start(f32[8,256]{1,0:T(8,128)S(1)} %reshape.28), channel_id=1, source_target_pairs={{0,8},{1,9},{2,10},{3,11},{4,12},{5,13},{6,14},{7,15},{8,0},{9,1},... | collective-permute-start | bytes 24584 | tf_op jit(solution)/shard_map/ppermute | solution.py:25
Sparse Core Ops, SparseCore 0:
  47.8 55.3 reduce-scatter.1
